TPU v7x, 128 devices: a whole 4x4x4 slice. The times are simulated.
128 devices in a mesh: row: 16 (over z, x), col: 8 (over y, core).
Axes of the slice: x: 4, y: 4, z: 4, core: 2. Of those that a mesh axis runs over, the one named last changes fastest.
Arguments:
- pole_values: float32 [65536], P('row'), may hold values from -32768 to 32768, as said below
- weights: float32 [65536], P('row'), may hold values from 0.15 to 0.5
- centers: float32 [65536], P('col'), as said below
- offsets: float32 [65536], P('col'), may hold values from -0.1 to 0.1
- chosen: int32 [2048], replicated, may hold values from 0 to 65535
- column_pole: int32 [2, 32768], P(None, 'row'), may hold values from 0 to 65535, as said below
- eigen_blocks: bfloat16 [6144, 2, 32768], P('col', None, 'row'), may hold values from -6 to 6
Outputs:
- roots_offset: float32 [65536], P('col')
- panel: float32 [6144, 2, 2048], P(('col', 'row'))
Inputs may be any that keep to these rules, and one draw needn't show every extreme that they name: `pole_values`: ascending; consecutive poles differ by 1/4 to 7/4; every pole is a multiple of 1/128. centers[i] is the midpoint of pole_values[i] and pole_values[i + 1]; the last one is the last pole plus 1/2. `chosen`: indices of roots. `column_pole`: each of 0 to 65535 stands once.
All inputs are finite; a program needn't handle non-finite values.
Results may differ from a plain program's by a relative error of at most 0.0021.
Values may be sent and summed in bfloat16 or wider, within the bound.
A program may use at most 128 MiB of HBM per device.

v0:
```python
import jax
import jax.numpy as jnp
from jax import lax
from jax.sharding import Mesh
from jax.sharding import PartitionSpec as P

ITERS = 3
ROW = ("row_0", "row_1")
COL_ROW = ("col", "row_0", "row_1")


def gather_turned(arrays, axis, dims):
    turned = [jnp.moveaxis(a, dim, 0) for a, dim in zip(arrays, dims)]
    widths = [t[0].size for t in turned]
    both = jnp.concatenate([t.reshape(-1, w) for t, w in zip(turned, widths)], axis=1)
    filled = lax.all_gather(both, axis, axis=0, tiled=True)
    blocks = jnp.split(filled, [sum(widths[:k]) for k in range(1, len(widths))], axis=1)
    return tuple(
        (
            jnp.moveaxis(b.reshape(-1, *t.shape[1:]), 0, dim)
            for b, t, dim in zip(blocks, turned, dims)
        )
    )


def copy_for_each(shard, axis):
    size = lax.axis_size(axis)
    return lax.all_to_all(
        jnp.broadcast_to(shard[None], (size, *shard.shape)), axis, 0, 0, tiled=True
    )


def joined_along(blocks, dim):
    blocks = jnp.moveaxis(blocks, 0, dim)
    lengths = blocks.shape
    return blocks.reshape(*lengths[:dim], lengths[dim] * lengths[dim + 1], *lengths[dim + 2 :])


def gather_directly(shard, axis, dim):
    blocks = copy_for_each(shard, axis)
    return joined_along(blocks, dim)


def by_axis(shard, axes):
    for axis in axes:
        shard = lax.psum(shard, axis)
    return shard


def block_sums(pole_vals, weight_sq, center_vals, offset_vals, block_rows):
    root_count = center_vals.shape[0]
    block_rows = min(block_rows, root_count)
    center_blocks = center_vals.reshape(root_count // block_rows, block_rows)
    offset_blocks = offset_vals.reshape(root_count // block_rows, block_rows)

    def per_block(blocks):
        distance = pole_vals[None, :] - blocks[0][:, None] - blocks[1][:, None]
        inverse = 1.0 / distance
        weighted = weight_sq[None, :] * inverse
        return (
            jnp.sum(weighted, axis=1),
            jnp.sum(weighted * inverse, axis=1),
            jnp.min(jnp.abs(distance), axis=1),
        )

    sums = lax.map(per_block, (center_blocks, offset_blocks))
    return tuple((item.reshape(root_count) for item in sums))


def newton_update(offset_now, sum_inverse, sum_square, nearest):
    limit = 0.5 * nearest
    return offset_now - jnp.clip((1.0 + sum_inverse) / sum_square, -limit, limit)


def cauchy_block(pole_picked, weight_picked, panel_center, panel_offset, inv_norm):
    distance = pole_picked[:, None] - panel_center[None, :] - panel_offset[None, :]
    return (weight_picked[:, None] * (1.0 / distance) * inv_norm[None, :]).astype(jnp.bfloat16)


def on_device(pole_values, weights, centers, offsets, chosen, column_pole, eigen_blocks):
    all_poles, all_weights = gather_turned((pole_values, weights), ROW, (0, 0))
    weight_sq = weights * weights
    per_device = offsets.shape[0] // lax.axis_size(ROW)
    first_root = lax.axis_index(ROW) * per_device
    my_centers = lax.dynamic_slice_in_dim(centers, first_root, per_device)
    my_offsets = lax.dynamic_slice_in_dim(offsets, first_root, per_device)
    all_sq = all_weights * all_weights
    for iteration in range(ITERS):
        sum_inverse, sum_square, nearest = block_sums(all_poles, all_sq, my_centers, my_offsets, 32)
        my_offsets = newton_update(my_offsets, sum_inverse, sum_square, nearest)
    offset_now = gather_directly(my_offsets, ROW, 0)
    full_centers, full_offsets = gather_turned((centers, offset_now), "col", (0, 0))
    panel_center = full_centers[chosen]
    panel_offset = full_offsets[chosen]
    partial_sq = block_sums(pole_values, weight_sq, panel_center, panel_offset, 64)[1]
    norm_sq = by_axis(partial_sq, ROW)
    inv_norm = lax.rsqrt(norm_sq)
    cauchy_halves = []
    for half_index in range(2):
        pole_index = column_pole[half_index]
        cauchy_halves.append(
            cauchy_block(
                all_poles[pole_index], all_weights[pole_index], panel_center, panel_offset, inv_norm
            )
        )
    panel = lax.psum_scatter(
        jnp.stack(
            [
                jnp.dot(
                    eigen_blocks[:, half_index, :],
                    cauchy_halves[half_index],
                    preferred_element_type=jnp.float32,
                )
                for half_index in range(2)
            ],
            axis=1,
        ),
        ROW,
        scatter_dimension=0,
        tiled=True,
    )
    return (offset_now, panel)


def solution(mesh):
    torus = Mesh(mesh.devices.reshape(4, 4, mesh.shape["col"]), ("row_0", "row_1", "col"))
    placed = (P(ROW), P(ROW), P("col"), P("col"), P(), P(None, ROW), P("col", None, ROW))
    return jax.shard_map(
        on_device,
        mesh=torus,
        in_specs=placed,
        out_specs=(P("col"), P(COL_ROW, None, None)),
        check_vma=False,
    )
```

profile of v0, /device:TPU:1, one launch (start us, length us, event | category | flops | bytes accessed | tf_op | source)
XLA Modules:
  0.0 557.3 jit_solution(9556216317746386524)
XLA Ops:
  9.6 21.0 %all_gather.6 = f32[65536,2]{0,1:T(2,128)S(1)} all-gather(f32[4096,2]{0,1:T(2,128)S(1)} %pad_maximum_fusion.2), channel_id=1, replica_groups=mesh['row_0'=4,'row_1'=4,'col'=8] {'row_0','row_1'}, dimensions={0}, use_global_device_ids=true | all-gather | bytes 557056 | tf_op jit(solution)/shard_map/all_gather | solution.py:16
  31.1 46.1 %while.52 = (s32[]{:T(128)}, f32[16,32]{1,0:T(8,128)S(1)}, f32[16,32]{1,0:T(8,128)S(1)}, f32[16,32]{1,0:T(8,128)S(1)}, f32[65536]{0:T(1024)S(1)}, /*index=5*/f32...) while((s32[]{:T(128)}, f32[16,32]{1,0:T(8,128)S(1)}, ...), condition=%wide.region_4.5_spmd, body=%wide.region_0.4_spmd.sunk | while | flops 18874272 | bytes 526325 | solution.py:66
  31.1 2.7 fusion.33
  34.0 2.7 fusion.33
  36.9 2.7 fusion.33
  39.8 2.7 fusion.33
  42.7 2.7 fusion.33
  45.5 2.7 fusion.33
  48.4 2.7 fusion.33
  51.3 2.7 fusion.33
  54.2 2.7 fusion.33
  57.0 2.7 fusion.33
  59.9 2.7 fusion.33
  62.8 2.7 fusion.33
  65.7 2.7 fusion.33
  68.6 2.7 fusion.33
  71.4 2.7 fusion.33
  74.3 2.7 fusion.33
  78.2 46.1 %while.53 = (s32[]{:T(128)}, f32[16,32]{1,0:T(8,128)S(1)}, f32[16,32]{1,0:T(8,128)S(1)}, f32[16,32]{1,0:T(8,128)S(1)}, f32[65536]{0:T(1024)S(1)}, /*index=5*/f32...) while((s32[]{:T(128)}, f32[16,32]{1,0:T(8,128)S(1)}, ...), condition=%wide.region_9.10_spmd, body=%wide.region_5.9_spmd.sunk | while | flops 18874272 | bytes 526325 | solution.py:66
  78.2 2.7 fusion.34
  81.1 2.7 fusion.34
  84.0 2.7 fusion.34
  86.9 2.7 fusion.34
  89.7 2.7 fusion.34
  92.6 2.7 fusion.34
  95.5 2.7 fusion.34
  98.4 2.7 fusion.34
  101.3 2.7 fusion.34
  104.1 2.7 fusion.34
  124.5 46.1 %while.54 = (s32[]{:T(128)}, f32[16,32]{1,0:T(8,128)S(1)}, f32[16,32]{1,0:T(8,128)S(1)}, f32[16,32]{1,0:T(8,128)S(1)}, f32[65536]{0:T(1024)S(1)}, /*index=5*/f32...) while((s32[]{:T(128)}, f32[16,32]{1,0:T(8,128)S(1)}, ...), condition=%wide.region_14.15_spmd, body=%wide.region_10.14_spmd.sunk | while | flops 18874272 | bytes 526325 | solution.py:66
  159.1 2.7 fusion.35
  171.4 4.7 all-to-all-start
  176.2 13.8 %fusion.26 = (bf16[768,1,2048]{2,1,0:T(2,128)(2,1)}, bf16[768,1,2048]{2,1,0:T(2,128)(2,1)}) fusion(bf16[768,2,2048]{2,1,0:T(2,128)(2,1)} %param.21), kind=kLoop, calls=%fused_computation.75 | loop fusion | bytes 12582912 | tf_op jit(solution)/shard_map/slice | solution.py:110
  190.1 11.8 %gather_fusion = f32[2048]{0:T(1024)S(1)} fusion(f32[65536]{0:T(1024)S(1)} %bitcast.100, s32[2048]{0:T(1024)S(1)} %broadcast_clamp_fusion.1), kind=kCustom, calls=%fused_computation | custom fusion | bytes 24576 | tf_op jit(solution)/shard_map/gather | solution.py:103
  201.9 11.8 %gather_fusion.1 = f32[2048]{0:T(1024)S(1)} fusion(f32[65536]{0:T(1024)S(1)} %bitcast.96, s32[2048]{0:T(1024)S(1)} %broadcast_clamp_fusion.1), kind=kCustom, calls=%fused_computation.1 | custom fusion | bytes 24576 | tf_op jit(solution)/shard_map/gather | solution.py:103
  213.7 11.8 %gather_fusion.5 = f32[2048]{0:T(1024)S(1)} fusion(f32[65536]{0:T(1024)S(1)} %bitcast.97, s32[2048]{0:T(1024)S(1)} %broadcast_clamp_fusion), kind=kCustom, calls=%fused_computation.5 | custom fusion | bytes 24576 | tf_op jit(solution)/shard_map/gather | solution.py:103
  225.5 11.8 %gather_fusion.4 = f32[2048]{0:T(1024)S(1)} fusion(f32[65536]{0:T(1024)S(1)} %bitcast.101, s32[2048]{0:T(1024)S(1)} %broadcast_clamp_fusion), kind=kCustom, calls=%fused_computation.4 | custom fusion | bytes 24576 | tf_op jit(solution)/shard_map/gather | solution.py:103
  237.4 19.6 %all_gather.7 = f32[65536,2]{0,1:T(2,128)S(1)} all-gather(f32[8192,2]{0,1:T(2,128)S(1)} %pad_maximum_fusion.1), channel_id=1, replica_groups=mesh['row_0'=4,'row_1'=4,'col'=8] {'col'}, dimensions={0}, use_global_device_ids=true | all-gather | bytes 589824 | tf_op jit(solution)/shard_map/all_gather | solution.py:16
  257.4 11.8 %gather_fusion.2 = f32[2048]{0:T(1024)S(1)} fusion(f32[65536]{0:T(1024)S(1)} %bitcast.103, s32[2048]{0:T(1024)S(1)} %fusion.23), kind=kCustom, calls=%fused_computation.2 | custom fusion | bytes 24576 | tf_op jit(solution)/shard_map/gather | solution.py:93
  269.3 11.8 %gather_fusion.3 = f32[2048]{0:T(1024)S(1)} fusion(f32[65536]{0:T(1024)S(1)} %bitcast.102, s32[2048]{0:T(1024)S(1)} %fusion.23), kind=kCustom, calls=%fused_computation.3 | custom fusion | bytes 24576 | tf_op jit(solution)/shard_map/gather | solution.py:94
  281.1 14.2 %while.55 = (s32[]{:T(128)}, f32[32,64]{1,0:T(8,128)S(1)}, f32[4096]{0:T(1024)S(1)}, f32[4096]{0:T(1024)S(1)}, f32[32,64]{1,0:T(8,128)S(1)}, /*index=5*/f32[32,64]{1,0:T(8,128)S(1)}, s32[]{:T(128)}, s32[]{:T(128)}) while((s32[]{:T(128)}, f32[32,64]{1,0:T(8,128)S(1)}, f32[4096]{0:T(1024)S(1)}, f32[4096]{0:T(1024)S(1)}, ...), condition=%wide.region_17.18_spmd, body=%wide.region_15.17_spmd.sunk | while | flops 1572802 | bytes 35165 | solution.py:66
  295.4 8.9 %psum.14 = f32[2048]{0:T(1024)S(1)} all-reduce(f32[2048]{0:T(1024)S(1)} %reshape.184), channel_id=1, replica_groups=mesh['row_0'=4,'row_1'=4,'col'=8] {'row_0'}, use_global_device_ids=true, to_apply=%region_18.19 | all-reduce | flops 2048 | bytes 16384 | tf_op jit(solution)/shard_map/psum | solution.py:46
  304.3 8.7 %psum.15 = f32[2048]{0:T(1024)S(1)} all-reduce(f32[2048]{0:T(1024)S(1)} %psum.14), channel_id=1, replica_groups=mesh['row_0'=4,'row_1'=4,'col'=8] {'row_1'}, use_global_device_ids=true, to_apply=%region_19.20 | all-reduce | flops 2048 | bytes 16384 | tf_op jit(solution)/shard_map/psum | solution.py:46
  313.0 14.9 %fusion.22 = f32[768,1,2048]{0,2,1:T(8,128)} fusion(f32[2048]{0:T(1024)S(1)} %rsqrt.3, f32[2048]{0:T(1024)S(1)} %gather_fusion.3, f32[2048]{0:T(1024)S(1)} %gather_fusion.2, f32[2048]{0:T(1024)S(1)} %gather_fusion.1, f32[2048]{0:T(1024)S(1)} %gather_fusion, bf16[768,1,2048]{2,1,0:T(2,128)(2,1)} %get-tuple-element.257), kind=kOutput, calls=%fused_computation.52 | convolution fusion | flops 6467616768 | bytes 9478144 | tf_op jit(solution)/shard_map/dot_general | solution.py:109
  327.9 12.2 %fusion.21 = f32[768,1,2048]{0,2,1:T(8,128)} fusion(f32[2048]{0:T(1024)S(1)} %gather_fusion.5, f32[2048]{0:T(1024)S(1)} %gather_fusion.4, f32[2048]{0:T(1024)S(1)} %rsqrt.3, f32[2048]{0:T(1024)S(1)} %gather_fusion.3, f32[2048]{0:T(1024)S(1)} %gather_fusion.2, bf16[768,1,2048]{2,1,0:T(2,128)(2,1)S(1)} %bitcast.105), kind=kOutput, calls=%fused_computation.51 | convolution fusion | flops 6467616768 | bytes 9478144 | tf_op jit(solution)/shard_map/dot_general | solution.py:109
  340.1 10.0 %pad_maximum_fusion = f32[768,2,2048]{0,2,1:T(8,128)} fusion(f32[768,1,2048]{0,2,1:T(8,128)} %fusion.21, f32[768,1,2048]{0,2,1:T(8,128)} %fusion.22), kind=kLoop, calls=%fused_computation.36 | loop fusion | flops 3145728 | bytes 25165824 | tf_op jit(solution)/shard_map/stack | solution.py:107
  350.1 19.4 %copy.18 = f32[768,2,2048]{2,1,0:T(2,128)} copy(f32[768,2,2048]{0,2,1:T(8,128)} %pad_maximum_fusion) | data formatting | bytes 25165824 | tf_op jit(solution)/shard_map/stack | solution.py:107
  371.4 176.4 %all-reduce.3.cloned.1.call-done = f32[768,2,2048]{2,1,0:T(2,128)} async-done(((f32[768,2,2048]{2,1,0:T(2,128)}), f32[768,2,2048]{2,1,0:T(2,128)}) %all-reduce.3.cloned.1.call-update) | async-done | bytes 12582928
  (377 shorter events, 86.3 us)
Async XLA Ops:
  7.2 169.0 %copy-start.4 = (s32[2048]{0:T(1024)S(1)}, s32[2048]{0:T(1024)}, u32[]{:S(2)}) copy-start(s32[2048]{0:T(1024)} %param.19) | copy-start | bytes 24580
  7.2 169.0 %copy-start.3 = (s32[2,2048]{1,0:T(2,128)S(1)}, s32[2,2048]{1,0:T(2,128)}, u32[]{:S(2)}) copy-start(s32[2,2048]{1,0:T(2,128)} %param.20) | copy-start | bytes 49156
  171.4 65.9 %all-to-all-start = ((f32[16,1,512]{2,1,0:T(1,128)}), f32[16,1,512]{2,1,0:T(1,128)S(1)}, u32[]{:S(2)}, u32[]{:S(2)}) async-start(f32[16,1,512]{2,1,0:T(1,128)} %broadcast_in_dim.72), calls=%async_computation | async-start | bytes 65536 | tf_op jit(solution)/shard_map/all_to_all | solution.py:28
  176.1 371.7 %all-reduce.3.cloned.1.call-start = ((), (), s32[]{:S(2)}) async-start(), calls=%async_computation.1 | async-start | bytes 25165824
  176.2 13.9 %copy-start.1 = (f32[4096]{0:T(1024)S(1)}, f32[4096]{0:T(1024)}, u32[]{:S(2)}) copy-start(f32[4096]{0:T(1024)} %param.16) | copy-start | bytes 49156
  213.7 23.6 %copy-start.2 = (f32[8192]{0:T(1024)S(1)}, f32[8192]{0:T(1024)}, u32[]{:S(2)}) copy-start(f32[8192]{0:T(1024)} %param.17) | copy-start | bytes 98308
  257.4 23.7 %copy-start = (f32[4096]{0:T(1024)S(1)}, f32[4096]{0:T(1024)}, u32[]{:S(2)}) copy-start(f32[4096]{0:T(1024)} %param.15) | copy-start | bytes 49156
  269.3 58.6 %slice-start = ((s8[6291456]{0:T(1024)(128)(4,1)}), s8[2097152]{0:T(1024)(128)(4,1)S(1)}, s32[]{:S(2)}) async-start(s8[6291456]{0:T(1024)(128)(4,1)} %bitcast.104), calls=%async_computation.2 | async-start | bytes 4194304
  313.0 14.9 %slice-start.1 = ((s8[6291456]{0:T(1024)(128)(4,1)}), s8[4194304]{0:T(1024)(128)(4,1)S(1)}, s32[]{:S(2)}) async-start(s8[6291456]{0:T(1024)(128)(4,1)} %bitcast.104), calls=%async_computation.3 | async-start | bytes 8388608
  369.5 0.7 copy-start.5
Sparse Core Ops, SparseCore 0:
  369.6 178.0 all-reduce.2
where the time goes:
time: 558 us; the launch traced here: 557 us
  waiting for transfers between devices  176 us (32%)
  other arithmetic  155 us (28%)
  local copies, waits for them, and re-layouts  119 us (21%)
  blocking collectives  58.2 us (10%)
  matrix products  27 us (5%)
  between operations  15 us (3%)
    unnamed x2, waiting for transfers between devices  176 us
    reduce_sum x80, other arithmetic, per_block(): jnp.sum(weighted * inverse, axis=1)  143 us
    all_gather x2, blocking collectives, gather_turned(): filled = lax.all_gather(both, axis, axis=0, tiled=True)  40.6 us
    dot_general x2, matrix products, on_device(): jnp.dot(eigen_blocks[:, half_index, :], cauchy_halves[half_index], prefer...  27 us
    gather x2, local copies, waits for them, and re-layouts, on_device(): all_weights[pole_index]  23.6 us
    gather x2, local copies, waits for them, and re-layouts, on_device(): all_poles[pole_index]  23.6 us
    another operation x1, local copies, waits for them, and re-layouts, on_device(): jnp.stack([jnp.dot(eigen_blocks[:, half_index, :], cauchy_halves[half_ind...  19.4 us
    psum x2, blocking collectives, by_axis(): shard = lax.psum(shard, axis)  17.6 us
  transfers between devices with their start and end apart: 2, of which 1 were waited for; matrix products, arithmetic and copies ran while one was open for 11% of the time, Pallas kernels for 0%

commit v1 on v0

--- a/solution.py
+++ b/solution.py
@@ -13,7 +13,9 @@
     turned = [jnp.moveaxis(a, dim, 0) for a, dim in zip(arrays, dims)]
     widths = [t[0].size for t in turned]
     both = jnp.concatenate([t.reshape(-1, w) for t, w in zip(turned, widths)], axis=1)
-    filled = lax.all_gather(both, axis, axis=0, tiled=True)
+    filled = jnp.concatenate(
+        lax.all_to_all(jnp.stack([both] * lax.axis_size(axis)), axis, 0, 0), axis=0
+    )
     blocks = jnp.split(filled, [sum(widths[:k]) for k in range(1, len(widths))], axis=1)
     return tuple(
         (

time: 558 us -> 540 us (0.968)
  blocking collectives: 58.2 us -> 14.2 us
  starting transfers between devices: 4.71 us -> 22.2 us
  waiting for transfers between devices: 176 us -> 184 us
    all_gather x2 -> x0, blocking collectives: 40.6 us -> none  [gather_turned(): filled = lax.all_gather(both, axis, axis=0, tiled=True)]
    all_to_all x0 -> x2, starting transfers between devices: none -> 15.5 us  [gather_turned(): lax.all_to_all(jnp.stack([both] * lax.axis_size(axis)), axis, 0, 0)]
    all_to_all x1, waiting for transfers between devices: 0.01 us -> 6.41 us  [copy_for_each(): lax.all_to_all(jnp.broadcast_to(shard[None], (size, *shard.shape)), axis,...]
  transfers between devices with their start and end apart: 2 -> 4, of which waited for: 1 -> 2; matrix products, arithmetic and copies ran while one was open for 11% -> 12% of each run, Pallas kernels for 0% -> 0%
where the time goes in v1:
time: 540 us; the launch traced here: 539 us
  waiting for transfers between devices  184 us (34%)
  other arithmetic  155 us (29%)
  local copies, waits for them, and re-layouts  120 us (22%)
  matrix products  27 us (5%)
  starting transfers between devices  22.2 us (4%)
  between operations  15 us (3%)
  blocking collectives  14.2 us (3%)
    unnamed x2, waiting for transfers between devices  177 us
    reduce_sum x80, other arithmetic, per_block(): jnp.sum(weighted * inverse, axis=1)  143 us
    dot_general x2, matrix products, on_device(): jnp.dot(eigen_blocks[:, half_index, :], cauchy_halves[half_index], prefer...  27 us
    gather x2, local copies, waits for them, and re-layouts, on_device(): all_weights[pole_index]  23.6 us
    gather x2, local copies, waits for them, and re-layouts, on_device(): all_poles[pole_index]  23.6 us
    another operation x1, local copies, waits for them, and re-layouts, on_device(): jnp.stack([jnp.dot(eigen_blocks[:, half_index, :], cauchy_halves[half_ind...  19.4 us
    all_to_all x2, starting transfers between devices, gather_turned(): lax.all_to_all(jnp.stack([both] * lax.axis_size(axis)), axis, 0, 0)  15.5 us
    psum x2, blocking collectives, by_axis(): shard = lax.psum(shard, axis)  14.2 us
  transfers between devices with their start and end apart: 4, of which 2 were waited for; matrix products, arithmetic and copies ran while one was open for 12% of the time, Pallas kernels for 0%

profile of v1, /device:TPU:1, one launch (start us, length us, event | category | flops | bytes accessed | tf_op | source)
XLA Modules:
  0.0 539.3 jit_solution(7366753288016299267)
XLA Ops:
  8.9 8.4 %all-to-all-start = ((f32[16,4096,2]{1,2,0:T(2,128)}), f32[16,4096,2]{1,2,0:T(2,128)S(1)}, u32[]{:S(2)}, u32[]{:S(2)}) async-start(f32[16,4096,2]{1,2,0:T(2,128)} %stack.10), calls=%async_computation | async-start | bytes 1048576 | tf_op jit(solution)/shard_map/all_to_all | solution.py:17
  17.4 13.8 %fusion.26 = (bf16[768,1,2048]{2,1,0:T(2,128)(2,1)}, bf16[768,1,2048]{2,1,0:T(2,128)(2,1)}) fusion(bf16[768,2,2048]{2,1,0:T(2,128)(2,1)} %param.21), kind=kLoop, calls=%fused_computation.75 | loop fusion | bytes 12582912 | tf_op jit(solution)/shard_map/slice | solution.py:112
  32.7 46.1 %while.52 = (s32[]{:T(128)}, f32[16,32]{1,0:T(8,128)S(1)}, f32[16,32]{1,0:T(8,128)S(1)}, f32[16,32]{1,0:T(8,128)S(1)}, f32[65536]{0:T(1024)S(1)}, /*index=5*/f32...) while((s32[]{:T(128)}, f32[16,32]{1,0:T(8,128)S(1)}, ...), condition=%wide.region_4.5_spmd, body=%wide.region_0.4_spmd.sunk | while | flops 18874272 | bytes 526325 | solution.py:68
  32.8 2.7 fusion.33
  35.6 2.7 fusion.33
  38.5 2.7 fusion.33
  41.4 2.7 fusion.33
  44.3 2.7 fusion.33
  47.2 2.7 fusion.33
  50.0 2.7 fusion.33
  52.9 2.7 fusion.33
  55.8 2.7 fusion.33
  58.7 2.7 fusion.33
  61.5 2.7 fusion.33
  64.4 2.7 fusion.33
  67.3 2.7 fusion.33
  70.2 2.7 fusion.33
  73.1 2.7 fusion.33
  75.9 2.7 fusion.33
  79.8 46.1 %while.53 = (s32[]{:T(128)}, f32[16,32]{1,0:T(8,128)S(1)}, f32[16,32]{1,0:T(8,128)S(1)}, f32[16,32]{1,0:T(8,128)S(1)}, f32[65536]{0:T(1024)S(1)}, /*index=5*/f32...) while((s32[]{:T(128)}, f32[16,32]{1,0:T(8,128)S(1)}, ...), condition=%wide.region_9.10_spmd, body=%wide.region_5.9_spmd.sunk | while | flops 18874272 | bytes 526325 | solution.py:68
  79.8 2.7 fusion.34
  82.7 2.7 fusion.34
  85.6 2.7 fusion.34
  88.5 2.7 fusion.34
  91.4 2.7 fusion.34
  94.2 2.7 fusion.34
  97.1 2.7 fusion.34
  100.0 2.7 fusion.34
  102.9 2.7 fusion.34
  126.2 46.1 %while.54 = (s32[]{:T(128)}, f32[16,32]{1,0:T(8,128)S(1)}, f32[16,32]{1,0:T(8,128)S(1)}, f32[16,32]{1,0:T(8,128)S(1)}, f32[65536]{0:T(1024)S(1)}, /*index=5*/f32...) while((s32[]{:T(128)}, f32[16,32]{1,0:T(8,128)S(1)}, ...), condition=%wide.region_14.15_spmd, body=%wide.region_10.14_spmd.sunk | while | flops 18874272 | bytes 526325 | solution.py:68
  169.4 2.7 fusion.35
  173.0 6.7 %all-to-all-start.1 = ((f32[16,1,512]{2,1,0:T(1,128)}), f32[16,1,512]{2,1,0:T(1,128)S(1)}, u32[]{:S(2)}, u32[]{:S(2)}) async-start(f32[16,1,512]{2,1,0:T(1,128)} %broadcast_in_dim.72), calls=%async_computation.1 | async-start | bytes 65536 | tf_op jit(solution)/shard_map/all_to_all | solution.py:30
  179.7 6.4 %all-to-all-done.1 = f32[16,1,512]{2,1,0:T(1,128)S(1)} async-done(((f32[16,1,512]{2,1,0:T(1,128)}), f32[16,1,512]{2,1,0:T(1,128)S(1)}, u32[]{:S(2)}, u32[]{:S(2)}) %all-to-all-start.1) | async-done | bytes 32800 | tf_op jit(solution)/shard_map/all_to_all | solution.py:30
  187.2 7.1 %all-to-all-start.2 = ((f32[8,8192,2]{1,2,0:T(2,128)}), f32[8,8192,2]{1,2,0:T(2,128)S(1)}, u32[]{:S(2)}, u32[]{:S(2)}) async-start(f32[8,8192,2]{1,2,0:T(2,128)} %stack.11), calls=%async_computation.2 | async-start | bytes 1048576 | tf_op jit(solution)/shard_map/all_to_all | solution.py:17
  194.4 11.8 %gather_fusion = f32[2048]{0:T(1024)S(1)} fusion(f32[65536]{0:T(1024)S(1)} %bitcast.102, s32[2048]{0:T(1024)S(1)} %broadcast_clamp_fusion.1), kind=kCustom, calls=%fused_computation | custom fusion | bytes 24576 | tf_op jit(solution)/shard_map/gather | solution.py:105
  206.2 11.8 %gather_fusion.1 = f32[2048]{0:T(1024)S(1)} fusion(f32[65536]{0:T(1024)S(1)} %bitcast.98, s32[2048]{0:T(1024)S(1)} %broadcast_clamp_fusion.1), kind=kCustom, calls=%fused_computation.1 | custom fusion | bytes 24576 | tf_op jit(solution)/shard_map/gather | solution.py:105
  217.9 11.8 %gather_fusion.5 = f32[2048]{0:T(1024)S(1)} fusion(f32[65536]{0:T(1024)S(1)} %bitcast.99, s32[2048]{0:T(1024)S(1)} %broadcast_clamp_fusion), kind=kCustom, calls=%fused_computation.5 | custom fusion | bytes 24576 | tf_op jit(solution)/shard_map/gather | solution.py:105
  229.7 11.8 %gather_fusion.4 = f32[2048]{0:T(1024)S(1)} fusion(f32[65536]{0:T(1024)S(1)} %bitcast.103, s32[2048]{0:T(1024)S(1)} %broadcast_clamp_fusion), kind=kCustom, calls=%fused_computation.4 | custom fusion | bytes 24576 | tf_op jit(solution)/shard_map/gather | solution.py:105
  242.0 11.8 %gather_fusion.2 = f32[2048]{0:T(1024)S(1)} fusion(f32[65536]{0:T(1024)S(1)} %bitcast.105, s32[2048]{0:T(1024)S(1)} %fusion.23), kind=kCustom, calls=%fused_computation.2 | custom fusion | bytes 24576 | tf_op jit(solution)/shard_map/gather | solution.py:95
  253.8 11.8 %gather_fusion.3 = f32[2048]{0:T(1024)S(1)} fusion(f32[65536]{0:T(1024)S(1)} %bitcast.104, s32[2048]{0:T(1024)S(1)} %fusion.23), kind=kCustom, calls=%fused_computation.3 | custom fusion | bytes 24576 | tf_op jit(solution)/shard_map/gather | solution.py:96
  265.7 14.2 %while.55 = (s32[]{:T(128)}, f32[32,64]{1,0:T(8,128)S(1)}, f32[4096]{0:T(1024)S(1)}, f32[4096]{0:T(1024)S(1)}, f32[32,64]{1,0:T(8,128)S(1)}, /*index=5*/f32[32,64]{1,0:T(8,128)S(1)}, s32[]{:T(128)}, s32[]{:T(128)}) while((s32[]{:T(128)}, f32[32,64]{1,0:T(8,128)S(1)}, f32[4096]{0:T(1024)S(1)}, f32[4096]{0:T(1024)S(1)}, ...), condition=%wide.region_17.18_spmd, body=%wide.region_15.17_spmd.sunk | while | flops 1572802 | bytes 35165 | solution.py:68
  279.9 7.0 %psum.14 = f32[2048]{0:T(1024)S(1)} all-reduce(f32[2048]{0:T(1024)S(1)} %reshape.196), channel_id=1, replica_groups=mesh['row_0'=4,'row_1'=4,'col'=8] {'row_0'}, use_global_device_ids=true, to_apply=%region_18.19 | all-reduce | flops 2048 | bytes 16384 | tf_op jit(solution)/shard_map/psum | solution.py:48
  286.9 7.2 %psum.15 = f32[2048]{0:T(1024)S(1)} all-reduce(f32[2048]{0:T(1024)S(1)} %psum.14), channel_id=1, replica_groups=mesh['row_0'=4,'row_1'=4,'col'=8] {'row_1'}, use_global_device_ids=true, to_apply=%region_19.20 | all-reduce | flops 2048 | bytes 16384 | tf_op jit(solution)/shard_map/psum | solution.py:48
  294.1 14.8 %fusion.22 = f32[768,1,2048]{0,2,1:T(8,128)} fusion(f32[2048]{0:T(1024)S(1)} %rsqrt.3, f32[2048]{0:T(1024)S(1)} %gather_fusion.3, f32[2048]{0:T(1024)S(1)} %gather_fusion.2, f32[2048]{0:T(1024)S(1)} %gather_fusion.1, f32[2048]{0:T(1024)S(1)} %gather_fusion, bf16[768,1,2048]{2,1,0:T(2,128)(2,1)} %get-tuple-element.257), kind=kOutput, calls=%fused_computation.52 | convolution fusion | flops 6467616768 | bytes 9478144 | tf_op jit(solution)/shard_map/dot_general | solution.py:111
  309.0 12.2 %fusion.21 = f32[768,1,2048]{0,2,1:T(8,128)} fusion(f32[2048]{0:T(1024)S(1)} %gather_fusion.5, f32[2048]{0:T(1024)S(1)} %gather_fusion.4, f32[2048]{0:T(1024)S(1)} %rsqrt.3, f32[2048]{0:T(1024)S(1)} %gather_fusion.3, f32[2048]{0:T(1024)S(1)} %gather_fusion.2, bf16[768,1,2048]{2,1,0:T(2,128)(2,1)S(1)} %bitcast.107), kind=kOutput, calls=%fused_computation.51 | convolution fusion | flops 6467616768 | bytes 9478144 | tf_op jit(solution)/shard_map/dot_general | solution.py:111
  321.2 10.0 %pad_maximum_fusion = f32[768,2,2048]{0,2,1:T(8,128)} fusion(f32[768,1,2048]{0,2,1:T(8,128)} %fusion.21, f32[768,1,2048]{0,2,1:T(8,128)} %fusion.22), kind=kLoop, calls=%fused_computation.36 | loop fusion | flops 3145728 | bytes 25165824 | tf_op jit(solution)/shard_map/stack | solution.py:109
  331.1 19.4 %copy.19 = f32[768,2,2048]{2,1,0:T(2,128)} copy(f32[768,2,2048]{0,2,1:T(8,128)} %pad_maximum_fusion) | data formatting | bytes 25165824 | tf_op jit(solution)/shard_map/stack | solution.py:109
  352.5 177.3 %all-reduce.3.cloned.1.call-done = f32[768,2,2048]{2,1,0:T(2,128)} async-done(((f32[768,2,2048]{2,1,0:T(2,128)}), f32[768,2,2048]{2,1,0:T(2,128)}) %all-reduce.3.cloned.1.call-update) | async-done | bytes 12582928
  (381 shorter events, 90.2 us)
Async XLA Ops:
  8.9 23.3 %all-to-all-start = ((f32[16,4096,2]{1,2,0:T(2,128)}), f32[16,4096,2]{1,2,0:T(2,128)S(1)}, u32[]{:S(2)}, u32[]{:S(2)}) async-start(f32[16,4096,2]{1,2,0:T(2,128)} %stack.10), calls=%async_computation | async-start | bytes 1048576 | tf_op jit(solution)/shard_map/all_to_all | solution.py:17
  17.4 13.9 %copy-start.2 = (f32[8192]{0:T(1024)S(1)}, f32[8192]{0:T(1024)}, u32[]{:S(2)}) copy-start(f32[8192]{0:T(1024)} %param.17) | copy-start | bytes 98308
  31.2 148.5 %copy-start.3 = (s32[2,2048]{1,0:T(2,128)S(1)}, s32[2,2048]{1,0:T(2,128)}, u32[]{:S(2)}) copy-start(s32[2,2048]{1,0:T(2,128)} %param.20) | copy-start | bytes 49156
  31.2 163.1 %copy-start.4 = (s32[2048]{0:T(1024)S(1)}, s32[2048]{0:T(1024)}, u32[]{:S(2)}) copy-start(s32[2048]{0:T(1024)} %param.19) | copy-start | bytes 24580
  31.2 163.1 %copy-start.1 = (f32[4096]{0:T(1024)S(1)}, f32[4096]{0:T(1024)}, u32[]{:S(2)}) copy-start(f32[4096]{0:T(1024)} %param.16) | copy-start | bytes 49156
  173.0 13.1 %all-to-all-start.1 = ((f32[16,1,512]{2,1,0:T(1,128)}), f32[16,1,512]{2,1,0:T(1,128)S(1)}, u32[]{:S(2)}, u32[]{:S(2)}) async-start(f32[16,1,512]{2,1,0:T(1,128)} %broadcast_in_dim.72), calls=%async_computation.1 | async-start | bytes 65536 | tf_op jit(solution)/shard_map/all_to_all | solution.py:30
  187.2 54.4 %all-to-all-start.2 = ((f32[8,8192,2]{1,2,0:T(2,128)}), f32[8,8192,2]{1,2,0:T(2,128)S(1)}, u32[]{:S(2)}, u32[]{:S(2)}) async-start(f32[8,8192,2]{1,2,0:T(2,128)} %stack.11), calls=%async_computation.2 | async-start | bytes 1048576 | tf_op jit(solution)/shard_map/all_to_all | solution.py:17
  194.3 335.5 %all-reduce.3.cloned.1.call-start = ((), (), s32[]{:S(2)}) async-start(), calls=%async_computation.3 | async-start | bytes 25165824
  241.9 23.7 %copy-start = (f32[4096]{0:T(1024)S(1)}, f32[4096]{0:T(1024)}, u32[]{:S(2)}) copy-start(f32[4096]{0:T(1024)} %param.15) | copy-start | bytes 49156
  253.8 55.2 %slice-start = ((s8[6291456]{0:T(1024)(128)(4,1)}), s8[2097152]{0:T(1024)(128)(4,1)S(1)}, s32[]{:S(2)}) async-start(s8[6291456]{0:T(1024)(128)(4,1)} %bitcast.106), calls=%async_computation.4 | async-start | bytes 4194304
  294.1 14.9 %slice-start.1 = ((s8[6291456]{0:T(1024)(128)(4,1)}), s8[4194304]{0:T(1024)(128)(4,1)S(1)}, s32[]{:S(2)}) async-start(s8[6291456]{0:T(1024)(128)(4,1)} %bitcast.106), calls=%async_computation.5 | async-start | bytes 8388608
  350.6 0.7 copy-start.5
Sparse Core Ops, SparseCore 0:
  350.7 178.9 all-reduce.2
